TPU v7x, 32 devices: a whole 2x2x4 slice. The times are simulated.
32 devices in a mesh: seq: 8 (over z, y), head: 4 (over x, core).
Axes of the slice: x: 2, y: 2, z: 4, core: 2. Of those that a mesh axis runs over, the one named last changes fastest.
Arguments:
- queries: bfloat16 [1024, 24576], P('seq', 'head'), may hold values from -325 to 325
- latents: bfloat16 [1024, 576], P('seq'), may hold values from -5 to 5
- doc_ids: int32 [1024], P('seq'), may hold values from 0 to 3, never falling along the last dimension, each value on 1 to 512 neighbouring positions
- key_weight: bfloat16 [512, 16384], P(None, 'head'), may hold values from -0.25 to 0.25
- value_weight: bfloat16 [512, 16384], P(None, 'head'), may hold values from -0.25 to 0.25
- out_grad: bfloat16 [1024, 16384], P('seq', 'head'), may hold values from -6 to 6
Outputs:
- attended: bfloat16 [1024, 16384], P('seq', 'head')
- latent_grad: float32 [1024, 576], P('seq')
- key_weight_grad: float32 [512, 16384], P('seq', 'head')
- value_weight_grad: float32 [512, 16384], P('seq', 'head')
Inputs may be any that keep to these rules, and one draw needn't show every extreme that they name: `doc_ids`: ids never fall along the sequence; every document holds 1 to 512 tokens, and one holds exactly that many.
All inputs are finite; a program needn't handle non-finite values.
Results may differ from a plain program's by a relative error of at most 0.028.
Values may be sent and summed in bfloat16 or wider, within the bound.
A program may use at most 128 MiB of HBM per device.

v0:
```python
import functools
import math

import jax
import jax.numpy as jnp
from jax import lax
from jax.experimental import pallas as pl
from jax.experimental.pallas import tpu as pltpu
from jax.sharding import PartitionSpec as P

NOPE = 128
ROPE = 64
VDIM = 128
LATENT = 512
REACH = 4
PAIR = 2
Y_LAG = 8
Z_LAG = 2
F_LAG = 3
MESH = pl.DeviceIdType.MESH
F32 = jnp.float32
BF16 = jnp.bfloat16


def dot(a, b, ca, cb):
    return lax.dot_general(a, b, (((ca,), (cb,)), ((), ())), preferred_element_type=F32)


def line_first(i, steps):
    return (i % 4 == 1) & (i < steps // 2)


def kernel(
    n, hn, steps, grid_steps, fin_lag,
    lat_ref, qid_ref, q_ref, g_ref, kw_ref, vw_ref,
    att_ref, lg_ref, kwg_ref, vwg_ref,
    latx, lat_all, lat_t, bias, lgacc, part, ry, rzp, rzm, ls, lr, hb,
    lat_ss, lat_rs, f_ss, f_rs, y_ss, y_rs, z_ss, zp_rs, zm_rs, l_ss, l_rs, h_ss, h_rs,
):
    j = pl.program_id(0)
    s = lax.axis_index("seq")
    h = lax.axis_index("head")
    line = n // 2
    z, y = s // 2, s % 2
    tok = lat_ref.shape[0]

    keys = (REACH + 1) * tok
    scale = 1.0 / math.sqrt(NOPE + ROPE)

    def lat_copy(d):
        return pltpu.make_async_remote_copy(
            src_ref=latx.at[h],
            dst_ref=lat_all.at[REACH - d, h],
            send_sem=lat_ss.at[d - 1], recv_sem=lat_rs.at[d - 1],
            device_id=(s + d, h), device_id_type=MESH,
        )

    def f_copy(d, k, slot):
        return pltpu.make_async_remote_copy(
            src_ref=lat_all.at[REACH - d, slot],
            dst_ref=lat_all.at[REACH - d, slot],
            send_sem=f_ss.at[k - 1, d - 1], recv_sem=f_rs.at[slot, d - 1],
            device_id=(s, (h + k) % hn), device_id_type=MESH,
        )

    def y_late_copy(i):
        return pltpu.make_async_remote_copy(
            src_ref=part.at[i, 1 - y, z], dst_ref=ry.at[i, 0],
            send_sem=y_ss.at[i], recv_sem=y_rs.at[i],
            device_id=(s + 1 - 2 * y, h), device_id_type=MESH,
        )

    def y_copy(i):
        return pltpu.make_async_remote_copy(
            src_ref=part.at[i, 1 - y], dst_ref=ry.at[i],
            send_sem=y_ss.at[i], recv_sem=y_rs.at[i],
            device_id=(s + 1 - 2 * y, h), device_id_type=MESH,
        )

    def z_copy(i, d, up, both):
        buf = rzp if up else rzm
        return pltpu.make_async_remote_copy(
            src_ref=part.at[i, :, d] if both else part.at[i, y, d],
            dst_ref=buf.at[i, :, d] if both else buf.at[i, y, d],
            send_sem=z_ss.at[i, d], recv_sem=(zp_rs if up else zm_rs).at[i, d],
            device_id=(s + 2 if up else s - 2, h), device_id_type=MESH,
        )

    def l_copy(d):
        return pltpu.make_async_remote_copy(
            src_ref=ls.at[d - 1], dst_ref=lr.at[d - 1],
            send_sem=l_ss.at[d - 1], recv_sem=l_rs.at[d - 1],
            device_id=(s - d, h), device_id_type=MESH,
        )

    def h_copy(k, slot):
        return pltpu.make_async_remote_copy(
            src_ref=hb.at[slot], dst_ref=hb.at[slot],
            send_sem=h_ss.at[k - 1], recv_sem=h_rs.at[slot],
            device_id=(s, (h + k) % hn), device_id_type=MESH,
        )

    @pl.when(j == 0)
    def _():
        ids = jnp.transpose(jnp.broadcast_to(qid_ref[...].astype(F32), (tok, tok)))
        lx = jnp.concatenate([lat_ref[...], ids[:, :latx.shape[2] - lat_ref.shape[1]].astype(BF16)], axis=1)
        latx[...] = lx.reshape(latx.shape)
        barrier = pltpu.get_barrier_semaphore()
        for d in range(1, REACH + 1):
            @pl.when(s + d < n)
            def _():
                pl.semaphore_signal(barrier, inc=1, device_id=(s + d, h), device_id_type=MESH)

            @pl.when(s - d >= 0)
            def _():
                pl.semaphore_signal(barrier, inc=1, device_id=(s - d, h), device_id_type=MESH)
        for k in range(1, hn):
            pl.semaphore_signal(barrier, inc=1, device_id=(s, (h + k) % hn), device_id_type=MESH)
        pl.semaphore_wait(barrier, jnp.minimum(s, REACH) + jnp.minimum(n - 1 - s, REACH) + hn - 1)
        for d in range(1, REACH + 1):
            @pl.when(s + d < n)
            def _():
                lat_copy(d).start()
        lat_all[REACH] = latx[...]
        lgacc[...] = jnp.zeros_like(lgacc)
        for d in range(1, REACH + 1):
            @pl.when(s - d >= 0)
            def _():
                lat_copy(d).wait_recv()
                for k in range(1, hn):
                    f_copy(d, k, h).start()

            @pl.when(s - d < 0)
            def _():
                lat_all[REACH - d] = jnp.zeros(lat_all.shape[1:], BF16)
        for d in range(1, REACH + 1):
            @pl.when(s - d >= 0)
            def _():
                for k in range(1, hn):
                    f_copy(d, k, (h + k) % hn).wait_recv()
        lat_t[...] = jnp.transpose(lat_all[...].reshape(keys, lat_all.shape[3])[:, :LATENT])
        key_row = lax.broadcasted_iota(jnp.int32, (keys, tok), 0)
        query_row = lax.broadcasted_iota(jnp.int32, (keys, tok), 1) + REACH * tok
        key_id = lat_all[...].reshape(keys, lat_all.shape[3])[:, LATENT + ROPE:LATENT + ROPE + 1].astype(F32)
        visible = (
            (key_row <= query_row)
            & (key_row >= (REACH - s) * tok)
            & (key_id == qid_ref[...].astype(F32))
        )
        bias[...] = jnp.where(visible, 0.0, -jnp.inf)

    @pl.when(j < steps)
    def _():
        lat_rows = lat_all[...].reshape(keys, lat_all.shape[3])
        lat = lat_rows[:, :LATENT]
        rope = lat_rows[:, LATENT:LATENT + ROPE]
        kw, vw = kw_ref[...], vw_ref[...]
        k2 = dot(lat, kw, 1, 0).astype(BF16)
        v2 = dot(lat, vw, 1, 0).astype(BF16)
        dks, dvs, rope_sum = [], [], None
        for a in range(PAIR):
            q = q_ref[:, a * (NOPE + ROPE):(a + 1) * (NOPE + ROPE)]
            g = g_ref[:, a * VDIM:(a + 1) * VDIM]
            v = v2[:, a * VDIM:(a + 1) * VDIM]
            k = jnp.concatenate([k2[:, a * NOPE:(a + 1) * NOPE], rope], axis=1)
            sc = dot(k, q, 1, 1) * scale + bias[...]
            e = jnp.exp(sc - jnp.max(sc, axis=0, keepdims=True))
            p = e * (1.0 / jnp.sum(e, axis=0, keepdims=True))
            pb = p.astype(BF16)
            att_ref[:, a * VDIM:(a + 1) * VDIM] = dot(pb, v, 0, 0).astype(BF16)
            dp = dot(v, g, 1, 1)
            delta = jnp.sum(pb.astype(F32) * dp, axis=0, keepdims=True)
            ds = (p * (dp - delta) * scale).astype(BF16)
            dk = dot(ds, q, 1, 0).astype(BF16)
            dvs.append(dot(pb, g, 1, 0).astype(BF16))
            dks.append(dk[:, :NOPE])
            r = dk[:, NOPE:].astype(F32)
            rope_sum = r if rope_sum is None else rope_sum + r
        dk2 = jnp.concatenate(dks, axis=1)
        dv2 = jnp.concatenate(dvs, axis=1)
        lgacc[:, :LATENT] += dot(dk2, kw, 1, 1) + dot(dv2, vw, 1, 1)
        lgacc[:, LATENT:] += rope_sum
        lt = lat_t[...]
        rows = part.shape[3]
        for col, dd in ((0, dk2), (PAIR * NOPE, dv2)):
            wg = dot(lt, dd, 1, 0).astype(BF16).reshape(line, 2, rows, dd.shape[1])
            for yy in range(2):
                part[j, yy, :, :, col:col + dd.shape[1]] = wg[:, yy]
        @pl.when(jnp.logical_not(line_first(j, steps)))
        def _():
            y_copy(j).start()

    @pl.when(j == steps - 1)
    def _():
        for d in range(1, REACH + 1):
            ls[d - 1] = lgacc[(REACH - d) * tok:(REACH - d + 1) * tok, :].astype(BF16)
        for d in range(1, REACH + 1):
            @pl.when(s - d >= 0)
            def _():
                l_copy(d).start()

    @pl.when(j == steps + 1)
    def _():
        for d in range(1, REACH + 1):
            @pl.when(s + d < n)
            def _():
                l_copy(d).wait_recv()
                lgacc[REACH * tok:, :] += lr[d - 1].astype(F32)
        hb[h] = lgacc[REACH * tok:, :].astype(BF16)
        for k in range(1, hn):
            h_copy(k, h).start()

    @pl.when(j == steps + 3)
    def _():
        for k in range(1, hn):
            h_copy(k, (h + k) % hn).wait_recv()
        total = hb[0].astype(F32)
        for k in range(1, hn):
            total = total + hb[k].astype(F32)
        lg_ref[...] = total

    iy = j - Y_LAG

    @pl.when((iy >= 0) & (iy < steps) & jnp.logical_not(line_first(iy, steps)))
    def _():
        y_copy(iy).wait_recv()
        part[iy, y] = (part[iy, y].astype(F32) + ry[iy].astype(F32)).astype(BF16)

    def hop(iz, pos, up, both):
        buf = rzp if up else rzm
        which = slice(None) if both else y
        for dist in range(1, line):
            d = z + dist if up else z - dist

            @pl.when((d < line) & (d >= 0))
            def _():
                @pl.when(pos > 0)
                def _():
                    z_copy(iz, d, up, both).wait_recv()
                    part[iz, which, d] = (part[iz, which, d].astype(F32) + buf[iz, which, d].astype(F32)).astype(BF16)
                z_copy(iz, d, up, both).start()

    for both in (True, False):
        for up in (True, False):
            pos = z if up else line - 1 - z
            iz = j - F_LAG * pos if both else j - Y_LAG - Z_LAG * pos

            @pl.when((iz >= 0) & (iz < steps) & (line_first(iz, steps) == both))
            def _():
                hop(iz, pos, up, both)

    il = j - F_LAG * (line - 1) - 1

    @pl.when((il >= 0) & (il < steps) & line_first(il, steps))
    def _():
        for up in (True, False):
            buf = rzp if up else rzm

            @pl.when(z > 0 if up else z < line - 1)
            def _():
                z_copy(il, z, up, True).wait_recv()
                part[il, :, z] = (part[il, :, z].astype(F32) + buf[il, :, z].astype(F32)).astype(BF16)
        y_late_copy(il).start()

    fin = j - fin_lag
    half = PAIR * NOPE

    @pl.when((fin >= 0) & (fin < steps))
    def _():
        own = part[fin, y, z].astype(F32)
        kwg_ref[...] = own[:, :half]
        vwg_ref[...] = own[:, half:]

        @pl.when(line_first(fin, steps))
        def _():
            y_late_copy(fin).wait_recv()
            got = ry[fin, 0].astype(F32)
            kwg_ref[...] += got[:, :half]
            vwg_ref[...] += got[:, half:]

        @pl.when(jnp.logical_not(line_first(fin, steps)))
        def _():
            for up in (True, False):
                buf = rzp if up else rzm

                @pl.when(z > 0 if up else z < line - 1)
                def _():
                    z_copy(fin, z, up, False).wait_recv()
                    got = buf[fin, y, z].astype(F32)
                    kwg_ref[...] += got[:, :half]
                    vwg_ref[...] += got[:, half:]

    @pl.when(j == grid_steps - 1)
    def _():
        for d in range(1, REACH + 1):
            @pl.when(s - d >= 0)
            def _():
                l_copy(d).wait_send()
        for k in range(1, hn):
            h_copy(k, h).wait_send()

        for d in range(1, REACH + 1):
            @pl.when(s + d < n)
            def _():
                lat_copy(d).wait_send()

            @pl.when(s - d >= 0)
            def _():
                for k in range(1, hn):
                    f_copy(d, k, h).wait_send()

        def drain(i, c):
            for both in (True, False):
                @pl.when(line_first(i, steps) == both)
                def _():
                    (y_late_copy if both else y_copy)(i).wait_send()
                    for d in range(line):
                        @pl.when(d != z)
                        def _():
                            z_copy(i, d, True, both).wait_send()
            return c

        lax.fori_loop(0, steps, drain, 0)


def per_device(n, hn, queries, latents, doc_ids, key_weight, value_weight, out_grad):
    tok = latents.shape[0]
    heads = key_weight.shape[1] // NOPE
    steps = heads // PAIR
    line = n // 2
    rows = LATENT // n
    lag = max(Y_LAG + Z_LAG * (line - 1), F_LAG * (line - 1) + 4)
    grid_steps = steps + max(lag, 4)
    keys = (REACH + 1) * tok
    width = LATENT + ROPE
    ids = doc_ids.reshape(1, tok)
    wide = width + 64
    whole = pl.BlockSpec(memory_space=pltpu.VMEM)

    def at(lag_by):
        return lambda j: (0, jnp.clip(j - lag_by, 0, steps - 1))

    dma = pltpu.SemaphoreType.DMA
    att, lg, kwg, vwg = pl.pallas_call(
        functools.partial(kernel, n, hn, steps, grid_steps, lag),
        grid=(grid_steps,),
        out_shape=(
            pltpu.HBM((tok, heads * VDIM), BF16),
            pltpu.HBM((tok, width), F32),
            pltpu.HBM((rows, heads * NOPE), F32),
            pltpu.HBM((rows, heads * VDIM), F32),
        ),
        in_specs=[
            whole,
            whole,
            pl.BlockSpec((tok, PAIR * (NOPE + ROPE)), at(0)),
            pl.BlockSpec((tok, PAIR * VDIM), at(0)),
            pl.BlockSpec((LATENT, PAIR * NOPE), at(0)),
            pl.BlockSpec((LATENT, PAIR * VDIM), at(0)),
        ],
        out_specs=(
            pl.BlockSpec((tok, PAIR * VDIM), at(0)),
            whole,
            pl.BlockSpec((rows, PAIR * NOPE), at(lag)),
            pl.BlockSpec((rows, PAIR * VDIM), at(lag)),
        ),
        scratch_shapes=[
            pltpu.VMEM((hn, tok // hn, wide), BF16),
            pltpu.VMEM((REACH + 1, hn, tok // hn, wide), BF16),
            pltpu.VMEM((LATENT, keys), BF16),
            pltpu.VMEM((keys, tok), F32),
            pltpu.VMEM((keys, width), F32),
            pltpu.VMEM((steps, 2, line, rows, PAIR * (NOPE + VDIM)), BF16),
            pltpu.VMEM((steps, line, rows, PAIR * (NOPE + VDIM)), BF16),
            pltpu.VMEM((steps, 2, line, rows, PAIR * (NOPE + VDIM)), BF16),
            pltpu.VMEM((steps, 2, line, rows, PAIR * (NOPE + VDIM)), BF16),
            pltpu.VMEM((REACH, tok, width), BF16),
            pltpu.VMEM((REACH, tok, width), BF16),
            pltpu.VMEM((hn, tok, width), BF16),
            dma((REACH,)), dma((REACH,)),
            dma((max(hn - 1, 1), REACH)), dma((hn, REACH)),
            dma((steps,)), dma((steps,)),
            dma((steps, line)), dma((steps, line)), dma((steps, line)),
            dma((REACH,)), dma((REACH,)),
            dma((max(hn - 1, 1),)), dma((hn,)),
        ],
        compiler_params=pltpu.CompilerParams(
            collective_id=0,
            has_side_effects=True,
            dimension_semantics=("arbitrary",),
            vmem_limit_bytes=60 * 1024 * 1024,
        ),
    )(latents, ids, queries, out_grad, key_weight, value_weight)
    return att, lg, kwg, vwg


def solution(mesh):
    in_specs = (
        P("seq", "head"),
        P("seq", None),
        P("seq"),
        P(None, "head"),
        P(None, "head"),
        P("seq", "head"),
    )
    out_specs = (P("seq", "head"), P("seq", None), P("seq", "head"), P("seq", "head"))
    body = functools.partial(per_device, mesh.shape["seq"], mesh.shape["head"])
    return jax.shard_map(
        body, mesh=mesh, in_specs=in_specs, out_specs=out_specs, check_vma=False
    )
```

profile of v0, /device:TPU:0, one launch (start us, length us, event | category | flops | bytes accessed | tf_op | source)
XLA Modules:
  0.0 159.0 jit_solution(10367154900210228906)
XLA Ops:
  0.6 1.7 %copy.10.lat_ref = bf16[128,576]{1,0:T(8,128)(2,1)} copy(bf16[128,576]{0,1:T(8,128)(2,1)} %param.7) | data formatting | bytes 294912 | tf_op args[1]
  2.3 149.2 %shard_map.93 = (bf16[128,4096]{1,0:T(8,128)(2,1)}, f32[128,576]{1,0:T(8,128)}, f32[64,4096]{1,0:T(8,128)}, f32[64,4096]{1,0:T(8,128)}) custom-call(bf16[128,576]{1,0:T(8,128)(2,1)} %copy.10.lat_ref, s32[1,128]{1,0:T(1,128)} %bitcast.1, bf16[128,6144]{1,0:T(8,128)(2,1)} %q_ref.1, bf16[128,4096]{1,0:T(8,128)(2,1)} %g_ref.1, bf16[512,4096]{1,0:T(8,128)(2,1)} %kw_ref.1, ...), custom_call_target="tpu_custom_call" | custom-call | tf_op jit(solution)/shard_map/pallas_call | solution.py:344
  151.6 0.0 copy-start
  151.6 1.9 %copy.11 = f32[128,576]{0,1:T(8,128)} copy(f32[128,576]{1,0:T(8,128)} %get-tuple-element.5) | data formatting | bytes 589824 | tf_op jit(solution)/shard_map/pallas_call | solution.py:344
  153.5 2.3 %copy.15 = bf16[128,4096]{1,0:T(8,128)(2,1)} copy(bf16[128,4096]{1,0:T(8,128)(2,1)} %get-tuple-element.12) | data formatting | bytes 2097152
  155.8 2.3 %copy.16 = f32[64,4096]{1,0:T(8,128)} copy(f32[64,4096]{1,0:T(8,128)} %get-tuple-element.14) | data formatting | bytes 2097152
  158.1 0.0 copy-done
  158.1 1.0 copy.17
Async XLA Ops:
  151.6 6.5 %copy-start = (f32[64,4096]{1,0:T(8,128)S(1)}, f32[64,4096]{1,0:T(8,128)}, u32[]{:S(2)}) copy-start(f32[64,4096]{1,0:T(8,128)} %get-tuple-element.15) | copy-start | bytes 3145732
where the time goes:
time: 159 us
  Pallas kernels  149 us (94%)
  local copies, waits for them, and re-layouts  9.17 us (6%)
    pallas_call x1, Pallas kernels, per_device(): pl.pallas_call(functools.partial(kernel, n, hn, steps, grid_steps, lag),...  149 us
    unnamed x6, local copies, waits for them, and re-layouts  7.24 us

commit v1 on v0

v1 whole, which is shorter than its diff:
```python
import functools
import math

import jax
import jax.numpy as jnp
from jax import lax
from jax.experimental import pallas as pl
from jax.experimental.pallas import tpu as pltpu
from jax.sharding import PartitionSpec as P

NOPE = 128
ROPE = 64
VDIM = 128
LATENT = 512
REACH = 4
PAIR = 2
NEAR = 3
FIN = 2
MESH = pl.DeviceIdType.MESH
F32 = jnp.float32
BF16 = jnp.bfloat16
BACK = REACH // 2
BLOCKS = 2 * (BACK + 1)
QW = PAIR * (NOPE + ROPE)
GW = PAIR * VDIM
WW = PAIR * (NOPE + VDIM)


def dot(a, b, ca, cb):
    return lax.dot_general(a, b, (((ca,), (cb,)), ((), ())), preferred_element_type=F32)


def lag_of(pos):
    return jnp.where(pos > 0, NEAR - 1 + pos, 0)


def kernel(
    n, hn, steps, turns, fin_lag,
    lat_ref, qid_ref, q_ref, g_ref, kw_ref, vw_ref,
    att_ref, lg_ref, kwg_ref, vwg_ref,
    lat_all, lat_t, bias, lgacc, wb, qb, gb, atts, part, rzp, rzm, yr, l1s, l1r, l2s, l2r, lgown, hb,
    w_ls, q_ls, g_ls, q_ss, q_rs, g_ss, g_rs, a_ss, a_rs,
    la_ss, la_rs, lb_ss, lb_rs, lc_ss, lc_rs,
    zp_ss, zm_ss, zp_rs, zm_rs, y_ss, y_rs, l1_ss, l1_rs, l2_ss, l2_rs, h_ss, h_rs,
):
    s = lax.axis_index("seq")
    h = lax.axis_index("head")
    line = n // 2
    z, y = s // 2, s % 2
    other = 1 - y
    mate = s + 1 - 2 * y
    core = h % 2
    twin = h + 1 - 2 * core
    tok = lat_ref.shape[1]
    width = LATENT + ROPE
    keys = BLOCKS * tok
    queries = 2 * tok
    own_heads = steps * PAIR
    to_log2 = 1.0 / math.log(2.0)
    scale = 1.0 / math.sqrt(NOPE + ROPE)

    def remote(src, dst, ss, rs, to):
        return pltpu.make_async_remote_copy(
            src_ref=src, dst_ref=dst, send_sem=ss, recv_sem=rs, device_id=to, device_id_type=MESH
        )

    def cols(half, j, wide):
        return pl.ds(pl.multiple_of(half * (steps * wide) + j * wide, 128), wide)

    def w_copy(j, which):
        ref, col, wide = (kw_ref, 0, PAIR * NOPE) if which == 0 else (vw_ref, PAIR * NOPE, GW)
        return pltpu.make_async_copy(
            ref.at[:, cols(y, j, wide)], wb.at[j, :, pl.ds(col, wide)], w_ls.at[j, which]
        )

    def q_own(j):
        return pltpu.make_async_copy(q_ref.at[:, cols(y, j, QW)], qb.at[j, 0], q_ls.at[j])

    def g_own(j):
        return pltpu.make_async_copy(g_ref.at[:, cols(y, j, GW)], gb.at[j, 0], g_ls.at[j])

    def q_swap(j):
        return remote(q_ref.at[:, cols(other, j, QW)], qb.at[j, 1], q_ss.at[j], q_rs.at[j], (mate, h))

    def g_swap(j):
        return remote(g_ref.at[:, cols(other, j, GW)], gb.at[j, 1], g_ss.at[j], g_rs.at[j], (mate, h))

    def a_swap(j, half):
        return remote(atts.at[j], att_ref.at[:, cols(half, j, GW)], a_ss.at[j], a_rs.at[j], (mate, h))

    def la_copy(k):
        to = mate if k == 0 else s + 2 * k
        return remote(
            lat_all.at[0, core], lat_all.at[1 if k == 0 else 2 * k, core], la_ss.at[k], la_rs.at[k], (to, h)
        )

    def lb_copy(k):
        return remote(
            lat_all.at[2 * k, core], lat_all.at[2 * k + 1, core], lb_ss.at[k - 1], lb_rs.at[k - 1], (mate, h)
        )

    def lc_copy(b, half):
        return remote(lat_all.at[b, half], lat_all.at[b, half], lc_ss.at[b - 1], lc_rs.at[b - 1], (s, twin))

    def z_copy(i, d, up):
        buf, ss, rs = (rzp, zp_ss, zp_rs) if up else (rzm, zm_ss, zm_rs)
        return remote(part.at[i, d], buf.at[i, d], ss.at[i, d], rs.at[i, d], (s + 2 if up else s - 2, h))

    def y_copy(i):
        return remote(part.at[i, z, other], yr.at[i], y_ss.at[i], y_rs.at[i], (mate, h))

    def l1_copy(k):
        return remote(l1s.at[(h + k) % hn], l1r.at[k - 1], l1_ss.at[k - 1], l1_rs.at[k - 1], (s, (h + k) % hn))

    def l2_copy(b):
        base = s if b % 2 == 0 else mate
        return remote(l2s.at[b - 1], l2r.at[b - 1], l2_ss.at[b - 1], l2_rs.at[b - 1], (base - 2 * (b // 2), h))

    def h_copy(k, slot):
        return remote(hb.at[slot], hb.at[slot], h_ss.at[k - 1], h_rs.at[slot], (s, (h + k) % hn))

    def enter():
        w_copy(0, 0).start()
        w_copy(0, 1).start()
        q_own(0).start()
        g_own(0).start()
        barrier = pltpu.get_barrier_semaphore()

        def greet(to):
            pl.semaphore_signal(barrier, inc=1, device_id=to, device_id_type=MESH)

        greet((mate, h))
        for k in range(1, BACK + 1):
            @pl.when(z + k < line)
            def _():
                greet((s + 2 * k, h))
                greet((mate + 2 * k, h))

            @pl.when(z - k >= 0)
            def _():
                greet((s - 2 * k, h))
                greet((mate - 2 * k, h))
        for k in range(1, hn):
            greet((s, (h + k) % hn))
        ids = jnp.transpose(jnp.broadcast_to(qid_ref[...].astype(F32), (tok, tok)))
        mine = jnp.transpose(lat_ref[...].astype(F32))
        packed = jnp.concatenate([mine, ids[:, :lat_all.shape[3] - width]], axis=1).astype(BF16)
        lat_all[0] = packed.reshape(lat_all.shape[1:])
        pl.semaphore_wait(barrier, 2 * (jnp.minimum(z, BACK) + jnp.minimum(line - 1 - z, BACK)) + hn)
        la_copy(0).start()
        for k in range(1, BACK + 1):
            @pl.when(z + k < line)
            def _():
                la_copy(k).start()
        q_swap(0).start()
        g_swap(0).start()

        def fetch(j, c):
            w_copy(j, 0).start()
            w_copy(j, 1).start()
            q_own(j).start()
            g_own(j).start()
            return c

        lax.fori_loop(1, steps, fetch, 0)
        lgacc[...] = jnp.zeros_like(lgacc)

        @pl.when(z == 0)
        def _():
            for i in range(steps):
                rzp[i, 0] = jnp.zeros(rzp.shape[2:], BF16)

        @pl.when(z == line - 1)
        def _():
            for i in range(steps):
                rzm[i, line - 1] = jnp.zeros(rzm.shape[2:], BF16)

        for k in range(1, BACK + 1):
            @pl.when(z - k >= 0)
            def _():
                la_copy(k).wait_recv()
                lb_copy(k).start()
                lc_copy(2 * k, core).start()

            @pl.when(z - k < 0)
            def _():
                for b in (2 * k, 2 * k + 1):
                    lat_all[b] = jnp.zeros(lat_all.shape[1:], BF16)
        la_copy(0).wait_recv()
        lc_copy(1, core).start()
        for k in range(1, BACK + 1):
            @pl.when(z - k >= 0)
            def _():
                lb_copy(k).wait_recv()
                lc_copy(2 * k + 1, core).start()

        def swap(j, c):
            q_swap(j).start()
            g_swap(j).start()
            return c

        lax.fori_loop(1, steps, swap, 0)
        lc_copy(1, 1 - core).wait_recv()
        for k in range(1, BACK + 1):
            @pl.when(z - k >= 0)
            def _():
                lc_copy(2 * k, 1 - core).wait_recv()
                lc_copy(2 * k + 1, 1 - core).wait_recv()
        rows = lat_all[...].reshape(keys, lat_all.shape[3])
        lat_t[...] = jnp.transpose(rows[:, :LATENT])
        mate_ids = jnp.transpose(rows[tok:2 * tok, LATENT:].astype(F32))[ROPE:ROPE + 1, :]
        row = lax.broadcasted_iota(jnp.int32, (tok, tok), 0)
        col = lax.broadcasted_iota(jnp.int32, (tok, tok), 1)
        for b in range(BLOCKS):
            block = (s if b % 2 == 0 else mate) - 2 * (b // 2)
            key_id = rows[b * tok:(b + 1) * tok, width:width + 1].astype(F32)
            for k in range(2):
                query_id = qid_ref[...].astype(F32) if k == 0 else mate_ids
                first = (s if k == 0 else mate) - block
                visible = (row <= col + first * tok) & (block >= 0) & (key_id == query_id)
                bias[b * tok:(b + 1) * tok, k * tok:(k + 1) * tok] = jnp.where(visible, 0.0, -jnp.inf)

    def compute(j):
        w_copy(j, 0).wait()
        w_copy(j, 1).wait()
        q_own(j).wait()
        g_own(j).wait()
        q_swap(j).wait_recv()
        g_swap(j).wait_recv()
        rows = lat_all[...].reshape(keys, lat_all.shape[3])
        lat = rows[:, :LATENT]
        rope = rows[:, LATENT:width]
        w = wb[j]
        q2 = qb[j].reshape(queries, QW)
        g2 = gb[j].reshape(queries, GW)
        kv = dot(lat, w, 1, 0).astype(BF16)
        dks, dvs, rope_sum = [], [], None
        for a in range(PAIR):
            q = q2[:, a * (NOPE + ROPE):(a + 1) * (NOPE + ROPE)]
            g = g2[:, a * VDIM:(a + 1) * VDIM]
            v = kv[:, PAIR * NOPE + a * VDIM:PAIR * NOPE + (a + 1) * VDIM]
            k = jnp.concatenate([kv[:, a * NOPE:(a + 1) * NOPE], rope], axis=1)
            sc = dot(k, q, 1, 1) * (scale * to_log2) + bias[...]
            e = jnp.exp2(sc - jnp.max(sc, axis=0, keepdims=True))
            p = e * (1.0 / jnp.sum(e, axis=0, keepdims=True))
            pb = p.astype(BF16)
            att = jnp.transpose(dot(v, pb, 0, 0)).astype(BF16)
            att_ref[:, pl.ds(pl.multiple_of((y * own_heads + j * PAIR + a) * VDIM, 128), VDIM)] = att[:tok]
            atts[j, :, a * VDIM:(a + 1) * VDIM] = att[tok:]
            dp = dot(v, g, 1, 1)
            delta = jnp.sum(p * dp, axis=0, keepdims=True)
            ds = (p * (dp - delta) * scale).astype(BF16)
            dk = dot(ds, q, 1, 0)
            dvs.append(dot(pb, g, 1, 0).astype(BF16))
            dks.append(dk[:, :NOPE].astype(BF16))
            r = dk[:, NOPE:]
            rope_sum = r if rope_sum is None else rope_sum + r
        dd = jnp.concatenate(dks + dvs, axis=1)
        part[j] = dot(lat_t[...], dd, 1, 0).astype(BF16).reshape(part.shape[1:])
        flat = lgacc.shape[:3]
        lgacc[:, :, :, :LATENT] += dot(dd, w, 1, 1).reshape(*flat, LATENT)
        lgacc[:, :, :, LATENT:] += rope_sum.reshape(*flat, ROPE)
        a_swap(j, y).start()

    def hop(i, pos, up):
        buf = rzp if up else rzm
        for dist in range(line - 1, 0, -1):
            d = z + dist if up else z - dist

            @pl.when((d < line) & (d >= 0))
            def _():
                @pl.when(pos > 0)
                def _():
                    z_copy(i, d, up).wait_recv()
                    part[i, d] = (part[i, d].astype(F32) + buf[i, d].astype(F32)).astype(BF16)
                z_copy(i, d, up).start()

    def finish(i):
        @pl.when(z > 0)
        def _():
            z_copy(i, z, True).wait_recv()

        @pl.when(z < line - 1)
        def _():
            z_copy(i, z, False).wait_recv()

        def total(yy):
            return part[i, z, yy].astype(F32) + rzp[i, z, yy].astype(F32) + rzm[i, z, yy].astype(F32)

        part[i, z, other] = total(other).astype(BF16)
        y_copy(i).start()
        put(i, y, total(y))

    def put(i, half, rows):
        kwg_ref[:, cols(half, i, PAIR * NOPE)] = rows[:, :PAIR * NOPE]
        vwg_ref[:, cols(half, i, GW)] = rows[:, PAIR * NOPE:]

    def close(i):
        y_copy(i).wait_recv()
        put(i, other, yr[i].astype(F32))

    def latent_send():
        for k in range(hn):
            l1s[k] = lgacc[:, k].astype(BF16)
        for k in range(1, hn):
            l1_copy(k).start()

    def latent_pass():
        for k in range(1, hn):
            l1_copy(k).wait_recv()
        for b in range(BLOCKS):
            tot = lgacc[b, h]
            for k in range(1, hn):
                tot = tot + l1r[k - 1, b].astype(F32)
            if b == 0:
                lgown[...] = tot
            else:
                l2s[b - 1] = tot.astype(BF16)
        for b in range(1, BLOCKS):
            @pl.when(z - b // 2 >= 0)
            def _():
                l2_copy(b).start()

    def latent_gather():
        for b in range(1, BLOCKS):
            @pl.when(z + b // 2 < line)
            def _():
                l2_copy(b).wait_recv()
                lgown[...] += l2r[b - 1].astype(F32)
        hb[h] = lgown[...].astype(BF16)
        for k in range(1, hn):
            h_copy(k, h).start()

    def latent_out():
        for k in range(1, hn):
            h_copy(k, (h + k) % hn).wait_recv()
        lg_ref[...] = jnp.transpose(hb[...].astype(F32).reshape(tok, width))

    enter()

    def turn(j, c):
        @pl.when(j < steps)
        def _():
            compute(j)

        @pl.when(j == steps - 1)
        def _():
            latent_send()

        for up in (True, False):
            pos = z if up else line - 1 - z
            i = j - lag_of(pos)

            @pl.when((i >= 0) & (i < steps))
            def _():
                hop(i, pos, up)

        @pl.when(j == steps + 1)
        def _():
            latent_pass()

        @pl.when(j == steps + 2)
        def _():
            latent_gather()

        i = j - fin_lag

        @pl.when((i >= 0) & (i < steps))
        def _():
            finish(i)

        @pl.when((i >= 1) & (i < steps + 1))
        def _():
            close(i - 1)

        return c

    lax.fori_loop(0, turns, turn, 0)
    latent_out()

    def drain(j, c):
        a_swap(j, other).wait_recv()
        a_swap(j, y).wait_send()
        q_swap(j).wait_send()
        g_swap(j).wait_send()
        y_copy(j).wait_send()
        for d in range(line):
            @pl.when(d > z)
            def _():
                z_copy(j, d, True).wait_send()

            @pl.when(d < z)
            def _():
                z_copy(j, d, False).wait_send()
        return c

    lax.fori_loop(0, steps, drain, 0)
    la_copy(0).wait_send()
    lc_copy(1, core).wait_send()
    for k in range(1, BACK + 1):
        @pl.when(z + k < line)
        def _():
            la_copy(k).wait_send()

        @pl.when(z - k >= 0)
        def _():
            lb_copy(k).wait_send()
            lc_copy(2 * k, core).wait_send()
            lc_copy(2 * k + 1, core).wait_send()
    for k in range(1, hn):
        l1_copy(k).wait_send()
        h_copy(k, h).wait_send()
    for b in range(1, BLOCKS):
        @pl.when(z - b // 2 >= 0)
        def _():
            l2_copy(b).wait_send()


def per_device(n, hn, queries, latents, doc_ids, key_weight, value_weight, out_grad):
    tok = latents.shape[0]
    heads = key_weight.shape[1] // NOPE
    steps = heads // 2 // PAIR
    line = n // 2
    rows = LATENT // n
    fin_lag = NEAR + line - 2 + FIN - 1
    turns = steps + max(fin_lag + 1, 3)
    keys = BLOCKS * tok
    width = LATENT + ROPE
    wide = width + 64
    share = tok // hn
    ids = doc_ids.reshape(1, tok)
    whole = pl.BlockSpec(memory_space=pltpu.VMEM)
    far = pl.BlockSpec(memory_space=pltpu.HBM)
    dma = pltpu.SemaphoreType.DMA
    ring = max(hn - 1, 1)
    att, lg, kwg, vwg = pl.pallas_call(
        functools.partial(kernel, n, hn, steps, turns, fin_lag),
        out_shape=(
            pltpu.VMEM((tok, heads * VDIM), BF16),
            pltpu.VMEM((width, tok), F32),
            pltpu.VMEM((rows, heads * NOPE), F32),
            pltpu.VMEM((rows, heads * VDIM), F32),
        ),
        in_specs=[whole, whole, far, far, far, far],
        out_specs=(whole, whole, whole, whole),
        scratch_shapes=[
            pltpu.VMEM((BLOCKS, 2, tok // 2, wide), BF16),
            pltpu.VMEM((LATENT, keys), BF16),
            pltpu.VMEM((keys, 2 * tok), F32),
            pltpu.VMEM((BLOCKS, hn, share, width), F32),
            pltpu.VMEM((steps, LATENT, WW), BF16),
            pltpu.VMEM((steps, 2, tok, QW), BF16),
            pltpu.VMEM((steps, 2, tok, GW), BF16),
            pltpu.VMEM((steps, tok, GW), BF16),
            pltpu.VMEM((steps, line, 2, rows, WW), BF16),
            pltpu.VMEM((steps, line, 2, rows, WW), BF16),
            pltpu.VMEM((steps, line, 2, rows, WW), BF16),
            pltpu.VMEM((steps, rows, WW), BF16),
            pltpu.VMEM((hn, BLOCKS, share, width), BF16),
            pltpu.VMEM((ring, BLOCKS, share, width), BF16),
            pltpu.VMEM((BLOCKS - 1, share, width), BF16),
            pltpu.VMEM((BLOCKS - 1, share, width), BF16),
            pltpu.VMEM((share, width), F32),
            pltpu.VMEM((hn, share, width), BF16),
            dma((steps, 2)), dma((steps,)), dma((steps,)),
            dma((steps,)), dma((steps,)), dma((steps,)), dma((steps,)), dma((steps,)), dma((steps,)),
            dma((BACK + 1,)), dma((BACK + 1,)), dma((BACK,)), dma((BACK,)), dma((BLOCKS - 1,)), dma((BLOCKS - 1,)),
            dma((steps, line)), dma((steps, line)), dma((steps, line)), dma((steps, line)),
            dma((steps,)), dma((steps,)),
            dma((ring,)), dma((ring,)), dma((BLOCKS - 1,)), dma((BLOCKS - 1,)), dma((ring,)), dma((hn,)),
        ],
        compiler_params=pltpu.CompilerParams(
            collective_id=0,
            has_side_effects=True,
            vmem_limit_bytes=48 * 1024 * 1024,
        ),
    )(latents.T, ids, queries, out_grad, key_weight, value_weight)
    return att, lg.T, kwg, vwg


def solution(mesh):
    in_specs = (
        P("seq", "head"),
        P("seq", None),
        P("seq"),
        P(None, "head"),
        P(None, "head"),
        P("seq", "head"),
    )
    out_specs = (P("seq", "head"), P("seq", None), P("seq", "head"), P("seq", "head"))
    body = functools.partial(per_device, mesh.shape["seq"], mesh.shape["head"])
    return jax.shard_map(
        body, mesh=mesh, in_specs=in_specs, out_specs=out_specs, check_vma=False
    )
```

time: 159 us -> 114 us (0.72)
  Pallas kernels: 149 us -> 105 us
    pallas_call x1, Pallas kernels: 149 us -> 105 us  [per_device(): pl.pallas_call(functools.partial(kernel, n, hn, steps, turns, fin_lag), o...]
    pallas_call x1 -> x0, local copies, waits for them, and re-layouts: 1.92 us -> none  [per_device(): pl.pallas_call(functools.partial(kernel, n, hn, steps, grid_steps, lag),...]
    unnamed x6 -> x12, local copies, waits for them, and re-layouts: 7.24 us -> 7.81 us
where the time goes in v1:
time: 114 us
  Pallas kernels  105 us (92%)
  local copies, waits for them, and re-layouts  7.81 us (7%)
    pallas_call x1, Pallas kernels, per_device(): pl.pallas_call(functools.partial(kernel, n, hn, steps, turns, fin_lag), o...  105 us
    unnamed x12, local copies, waits for them, and re-layouts  7.81 us

profile of v1, /device:TPU:0, one launch (start us, length us, event | category | flops | bytes accessed | tf_op | source)
XLA Modules:
  0.0 113.9 jit_solution(7861954604659927693)
XLA Ops:
  0.6 0.0 copy-start
  0.6 1.4 %copy-done = bf16[128,6144]{1,0:T(8,128)(2,1)S(1)} copy-done((bf16[128,6144]{1,0:T(8,128)(2,1)S(1)}, bf16[128,6144]{1,0:T(8,128)(2,1)}, u32[]{:S(2)}) %copy-start) | copy-done | bytes 1572888
  2.0 0.0 copy-start.1
  2.0 1.2 %copy-done.1 = bf16[128,4096]{1,0:T(8,128)(2,1)S(1)} copy-done((bf16[128,4096]{1,0:T(8,128)(2,1)S(1)}, bf16[128,4096]{1,0:T(8,128)(2,1)}, u32[]{:S(2)}) %copy-start.1) | copy-done | bytes 1048600
  3.3 0.0 copy-start.2
  3.3 0.9 copy-done.2
  4.2 0.0 copy-start.3
  4.2 0.7 copy-done.3
  4.8 105.4 %shard_map.93 = (bf16[128,4096]{1,0:T(8,128)(2,1)S(1)}, f32[576,128]{1,0:T(8,128)S(1)}, f32[64,4096]{1,0:T(8,128)S(1)}, f32[64,4096]{1,0:T(8,128)S(1)}) custom-call(bf16[576,128]{1,0:T(8,128)(2,1)S(1)} %bitcast.4, s32[1,128]{1,0:T(1,128)S(1)} %bitcast.5, bf16[128,6144]{1,0:T(8,128)(2,1)S(1)} %copy-done, bf16[128,4096]{1,0:T(8,128)(2,1)S(1)} %copy-done.1, ...), custom_call_target="tpu_custom_call" | custom-call | tf_op jit(solution)/shard_map/pallas_call | solution.py:436
  110.2 1.0 copy.14
  111.2 0.7 copy.15
  111.9 1.0 copy.16
  112.9 1.0 copy.17
Async XLA Ops:
  0.6 1.4 %copy-start = (bf16[128,6144]{1,0:T(8,128)(2,1)S(1)}, bf16[128,6144]{1,0:T(8,128)(2,1)}, u32[]{:S(2)}) copy-start(bf16[128,6144]{1,0:T(8,128)(2,1)} %q_ref.1) | copy-start | bytes 4718596
  2.0 1.2 %copy-start.1 = (bf16[128,4096]{1,0:T(8,128)(2,1)S(1)}, bf16[128,4096]{1,0:T(8,128)(2,1)}, u32[]{:S(2)}) copy-start(bf16[128,4096]{1,0:T(8,128)(2,1)} %g_ref.1) | copy-start | bytes 3145732
  3.3 0.9 copy-start.2
  4.2 0.7 copy-start.3

commit v2 on v1

--- a/solution.py
+++ b/solution.py
@@ -15,6 +15,7 @@
 REACH = 4
 PAIR = 2
 NEAR = 3
+VMEM_LIMIT = 60 * 1024 * 1024
 FIN = 2
 MESH = pl.DeviceIdType.MESH
 F32 = jnp.float32
@@ -36,10 +37,10 @@
 
 def kernel(
     n, hn, steps, turns, fin_lag,
-    lat_ref, qid_ref, q_ref, g_ref, kw_ref, vw_ref,
+    lat_hbm, qid_hbm, q_ref, g_ref, kw_ref, vw_ref,
     att_ref, lg_ref, kwg_ref, vwg_ref,
-    lat_all, lat_t, bias, lgacc, wb, qb, gb, atts, part, rzp, rzm, yr, l1s, l1r, l2s, l2r, lgown, hb,
-    w_ls, q_ls, g_ls, q_ss, q_rs, g_ss, g_rs, a_ss, a_rs,
+    lat_ref, qid_ref, lat_all, lat_t, bias, lgacc, wb, qb, gb, atts, part, rzp, rzm, yr, l1s, l1r, l2s, l2r, lgown, hb,
+    in_ls, w_ls, q_ls, g_ls, q_ss, q_rs, g_ss, g_rs, a_ss, a_rs,
     la_ss, la_rs, lb_ss, lb_rs, lc_ss, lc_rs,
     zp_ss, zm_ss, zp_rs, zm_rs, y_ss, y_rs, l1_ss, l1_rs, l2_ss, l2_rs, h_ss, h_rs,
 ):
@@ -120,6 +121,12 @@
         return remote(hb.at[slot], hb.at[slot], h_ss.at[k - 1], h_rs.at[slot], (s, (h + k) % hn))
 
     def enter():
+        loads = [
+            pltpu.make_async_copy(src, dst, in_ls.at[k])
+            for k, (src, dst) in enumerate(((lat_hbm, lat_ref), (qid_hbm, qid_ref)))
+        ]
+        for load in loads:
+            load.start()
         w_copy(0, 0).start()
         w_copy(0, 1).start()
         q_own(0).start()
@@ -142,6 +149,8 @@
                 greet((mate - 2 * k, h))
         for k in range(1, hn):
             greet((s, (h + k) % hn))
+        for load in loads:
+            load.wait()
         ids = jnp.transpose(jnp.broadcast_to(qid_ref[...].astype(F32), (tok, tok)))
         mine = jnp.transpose(lat_ref[...].astype(F32))
         packed = jnp.concatenate([mine, ids[:, :lat_all.shape[3] - width]], axis=1).astype(BF16)
@@ -416,6 +425,15 @@
             l2_copy(b).wait_send()
 
 
+def flush(*refs):
+    sems = refs[-1]
+    copies = [pltpu.make_async_copy(refs[k], refs[4 + k], sems.at[k]) for k in range(4)]
+    for copy in copies:
+        copy.start()
+    for copy in copies:
+        copy.wait()
+
+
 def per_device(n, hn, queries, latents, doc_ids, key_weight, value_weight, out_grad):
     tok = latents.shape[0]
     heads = key_weight.shape[1] // NOPE
@@ -441,9 +459,11 @@
             pltpu.VMEM((rows, heads * NOPE), F32),
             pltpu.VMEM((rows, heads * VDIM), F32),
         ),
-        in_specs=[whole, whole, far, far, far, far],
+        in_specs=[far] * 6,
         out_specs=(whole, whole, whole, whole),
         scratch_shapes=[
+            pltpu.VMEM((width, tok), BF16),
+            pltpu.VMEM((1, tok), jnp.int32),
             pltpu.VMEM((BLOCKS, 2, tok // 2, wide), BF16),
             pltpu.VMEM((LATENT, keys), BF16),
             pltpu.VMEM((keys, 2 * tok), F32),
@@ -462,7 +482,7 @@
             pltpu.VMEM((BLOCKS - 1, share, width), BF16),
             pltpu.VMEM((share, width), F32),
             pltpu.VMEM((hn, share, width), BF16),
-            dma((steps, 2)), dma((steps,)), dma((steps,)),
+            dma((2,)), dma((steps, 2)), dma((steps,)), dma((steps,)),
             dma((steps,)), dma((steps,)), dma((steps,)), dma((steps,)), dma((steps,)), dma((steps,)),
             dma((BACK + 1,)), dma((BACK + 1,)), dma((BACK,)), dma((BACK,)), dma((BLOCKS - 1,)), dma((BLOCKS - 1,)),
             dma((steps, line)), dma((steps, line)), dma((steps, line)), dma((steps, line)),
@@ -472,9 +492,18 @@
         compiler_params=pltpu.CompilerParams(
             collective_id=0,
             has_side_effects=True,
-            vmem_limit_bytes=48 * 1024 * 1024,
+            vmem_limit_bytes=VMEM_LIMIT,
         ),
     )(latents.T, ids, queries, out_grad, key_weight, value_weight)
+    out = (att, lg, kwg, vwg)
+    att, lg, kwg, vwg = pl.pallas_call(
+        flush,
+        out_shape=tuple(pltpu.HBM(o.shape, o.dtype) for o in out),
+        in_specs=[whole] * 4,
+        out_specs=(far,) * 4,
+        scratch_shapes=[dma((4,))],
+        compiler_params=pltpu.CompilerParams(vmem_limit_bytes=1024 * 1024),
+    )(*out)
     return att, lg.T, kwg, vwg
 
 

time: 114 us -> 108 us (0.947)
  local copies, waits for them, and re-layouts: 7.81 us -> 0 us
  Pallas kernels: 105 us -> 107 us
    unnamed x12 -> x0, local copies, waits for them, and re-layouts: 7.81 us -> none
    pallas_call x0 -> x1, Pallas kernels: none -> 1.8 us  [per_device(): pl.pallas_call(flush, out_shape=tuple((pltpu.HBM(o.shape, o.dtype) for o...]
where the time goes in v2:
time: 108 us
  Pallas kernels  107 us (99%)
    pallas_call x1, Pallas kernels, per_device(): pl.pallas_call(functools.partial(kernel, n, hn, steps, turns, fin_lag), o...  105 us

profile of v2, /device:TPU:0, one launch (start us, length us, event | category | flops | bytes accessed | tf_op | source)
XLA Modules:
  0.0 107.9 jit_solution(10467385451395633750)
XLA Ops:
  0.6 105.4 %shard_map.93 = (bf16[128,4096]{1,0:T(8,128)(2,1)S(1)}, f32[576,128]{1,0:T(8,128)S(1)}, f32[64,4096]{1,0:T(8,128)S(1)}, f32[64,4096]{1,0:T(8,128)S(1)}) custom-call(bf16[576,128]{1,0:T(8,128)(2,1)} %bitcast.3, s32[1,128]{1,0:T(1,128)} %bitcast.4, bf16[128,6144]{1,0:T(8,128)(2,1)} %q_ref.1, bf16[128,4096]{1,0:T(8,128)(2,1)} %g_ref.1, ...), custom_call_target="tpu_custom_call" | custom-call | tf_op jit(solution)/shard_map/pallas_call | solution.py:454
  106.1 1.8 %shard_map.94 = (bf16[128,4096]{1,0:T(8,128)(2,1)}, f32[576,128]{1,0:T(8,128)}, f32[64,4096]{1,0:T(8,128)}, f32[64,4096]{1,0:T(8,128)}) custom-call(bf16[128,4096]{1,0:T(8,128)(2,1)S(1)} %get-tuple-element.12.refs_0_, f32[576,128]{1,0:T(8,128)S(1)} %get-tuple-element.13.refs_1_, f32[64,4096]{1,0:T(8,128)S(1)} %get-tuple-element.14.refs_2_, ...), custom_call_target="tpu_custom_call" | custom-call | tf_op jit(solution)/shard_map/pallas_call | solution.py:499

commit v3 on v2

v3 whole, which is shorter than its diff:
```python
import functools
import math

import jax
import jax.numpy as jnp
from jax import lax
from jax.experimental import pallas as pl
from jax.experimental.pallas import tpu as pltpu
from jax.sharding import PartitionSpec as P

NOPE = 128
ROPE = 64
VDIM = 128
LATENT = 512
REACH = 4
PAIR = 2
LEND = 3
LATE = 2
VMEM_LIMIT = 60 * 1024 * 1024
MESH = pl.DeviceIdType.MESH
F32 = jnp.float32
BF16 = jnp.bfloat16
BACK = REACH // 2
BLOCKS = 2 * (BACK + 1)
SPAN = BLOCKS + 2
QW = PAIR * (NOPE + ROPE)
GW = PAIR * VDIM
WW = PAIR * (NOPE + VDIM)


def dot(a, b, ca, cb):
    return lax.dot_general(a, b, (((ca,), (cb,)), ((), ())), preferred_element_type=F32)


def pick(table, t):
    out = jnp.int32(0)
    for k, v in enumerate(table):
        if v:
            out = out + jnp.where(t == k, v, 0)
    return out


def plan(chunks, line):
    lent = max(1, chunks * LEND // 8)
    plain = chunks - lent
    late = min(LATE, plain)
    order = [("L", c) for c in range(max(1, lent - 1))] + [("N", lent)]
    order += [("L", c) for c in range(max(1, lent - 1), lent)] + [("N", c) for c in range(lent + 1, chunks)]
    turns, ready, own = [], {}, {}
    for kind, c in order:
        own[c] = len(turns)
        turns.append((c, 0))
        if kind == "L":
            turns.append((c, 1))
        ready[c] = len(turns) - 1
    work = len(turns)
    tail = work - 1 + max(late * (line - 2), 2 * (line - 3) + late - 1) + 1
    done = {}
    for c in range(chunks):
        late_rank = c - (chunks - late)
        done[c] = ready[c] + 2 * (line - 2) if late_rank < 0 else tail + late_rank
    return lent, plain, late, turns, ready, [c for _, c in order], done


def kernel(
    n, hn, chunks,
    lat_hbm, qid_hbm, q_ref, g_ref, kw_ref, vw_ref,
    att_ref, lg_ref, kwg_ref, vwg_ref,
    lat_ref, qid_ref, lat_all, lat_t, bias, lgacc, wb, qb, gb, atts, part, rzp, rzm, yr,
    l1s, l1r, twos, xs, xr, l2s, l2r, lgown, hb,
    in_ls, w_ls, q_ls, g_ls, q_ss, q_rs, g_ss, g_rs, qe_ss, qe_rs, ge_ss, ge_rs, a_ss, a_rs, ae_rs,
    la_ss, la_rs, lb_ss, lb_rs, lc_ss, lc_rs,
    zp_ss, zm_ss, zp_rs, zm_rs, y_ss, y_rs, l1_ss, l1_rs, x_ss, x_rs, l2_ss, l2_rs, h_ss, h_rs,
):
    s = lax.axis_index("seq")
    h = lax.axis_index("head")
    line = n // 2
    lent, plain, late, turns, ready, order, done = plan(chunks, line)
    work = len(turns)
    z, y = s // 2, s % 2
    other = 1 - y
    mate = s + 1 - 2 * y
    core = h % 2
    twin = h + 1 - 2 * core
    chips = hn // 2
    chip = h // 2
    tok = lat_ref.shape[1]
    width = LATENT + ROPE
    keys = BLOCKS * tok
    queries = 2 * tok
    to_log2 = 1.0 / math.log(2.0)
    scale = 1.0 / math.sqrt(NOPE + ROPE)
    low, high = z == 0, z == line - 1
    edge = low | high
    inner = jnp.logical_not(edge)
    borrows_low, borrows_high = z == 1, z == line - 2
    borrows = borrows_low | borrows_high
    step = jnp.where(low | borrows_high, 2, -2)

    def remote(src, dst, ss, rs, to):
        return pltpu.make_async_remote_copy(
            src_ref=src, dst_ref=dst, send_sem=ss, recv_sem=rs, device_id=to, device_id_type=MESH
        )

    def cols(half, j, wide):
        return pl.ds(pl.multiple_of(half * (chunks * wide) + j * wide, 128), wide)

    def w_copy(j, which):
        ref, col, wide = (kw_ref, 0, PAIR * NOPE) if which == 0 else (vw_ref, PAIR * NOPE, GW)
        return pltpu.make_async_copy(
            ref.at[:, cols(y, j, wide)], wb.at[j, :, pl.ds(col, wide)], w_ls.at[j, which]
        )

    def q_own(j):
        return pltpu.make_async_copy(q_ref.at[:, cols(y, j, QW)], qb.at[j, 0], q_ls.at[j])

    def g_own(j):
        return pltpu.make_async_copy(g_ref.at[:, cols(y, j, GW)], gb.at[j, 0], g_ls.at[j])

    def q_swap(j):
        return remote(q_ref.at[:, cols(other, j, QW)], qb.at[j, 1], q_ss.at[j], q_rs.at[j], (mate, h))

    def g_swap(j):
        return remote(g_ref.at[:, cols(other, j, GW)], gb.at[j, 1], g_ss.at[j], g_rs.at[j], (mate, h))

    def q_lend(c, k):
        src = q_ref.at[:, cols(y, c, QW)] if k == 0 else qb.at[c, 1]
        return remote(src, qb.at[chunks + c, k], qe_ss.at[c, k], qe_rs.at[c, k], (s + step, h))

    def g_lend(c, k):
        src = g_ref.at[:, cols(y, c, GW)] if k == 0 else gb.at[c, 1]
        return remote(src, gb.at[chunks + c, k], ge_ss.at[c, k], ge_rs.at[c, k], (s + step, h))

    def a_swap(j, half):
        return remote(atts.at[j, 1], att_ref.at[:, cols(half, j, GW)], a_ss.at[j, 1], a_rs.at[j], (mate, h))

    def a_lent(c, k):
        return remote(atts.at[chunks + c, k], atts.at[c, k], a_ss.at[chunks + c, k], ae_rs.at[c, k], (s + step, h))

    def la_copy(k):
        to, b = (mate, 3) if k == 0 else (s + 2 * k, 2 * (k + 1))
        return remote(lat_all.at[2, core], lat_all.at[b, core], la_ss.at[k + 1], la_rs.at[k + 1], (to, h))

    def lb_copy(k):
        b = 2 * (k + 1)
        return remote(lat_all.at[b, core], lat_all.at[b + 1, core], lb_ss.at[k + 1], lb_rs.at[k + 1], (mate, h))

    def lc_copy(b, half):
        return remote(lat_all.at[b, half], lat_all.at[b, half], lc_ss.at[b], lc_rs.at[b], (s, twin))

    def sends_to(k):
        return high if k < 0 else z + k < line

    def gets_from(k):
        return borrows_high if k < 0 else z - k >= 0

    PAIRS = [p for p in range(SPAN // 2 - 1, -1, -1) if p != 1] + [1]
    FAR = [k for k in range(-1, BACK + 1) if k != 0]

    def z_copy(i, d, up):
        buf, ss, rs = (rzp, zp_ss, zp_rs) if up else (rzm, zm_ss, zm_rs)
        return remote(part.at[i, d], buf.at[i, d], ss.at[i, d], rs.at[i, d], (s + 2 if up else s - 2, h))

    def y_copy(i):
        return remote(part.at[i, z, other], yr.at[i], y_ss.at[i], y_rs.at[i], (mate, h))

    def l1_copy():
        return remote(l1s, l1r, l1_ss.at[0], l1_rs.at[0], (s, twin))

    def x_copy(k, p):
        at = pl.ds(2 * p, 2)
        return remote(
            xs.at[k - 1, at], xr.at[k - 1, at], x_ss.at[k - 1, p], x_rs.at[k - 1, p], (s, (h + 2 * k) % hn)
        )

    def l2_copy(b):
        base = s if b % 2 == 0 else mate
        return remote(l2s.at[b], l2r.at[b], l2_ss.at[b], l2_rs.at[b], (base - 2 * (b // 2 - 1), h))

    def h_copy(k, slot):
        return remote(hb.at[slot], hb.at[slot], h_ss.at[k - 1], h_rs.at[slot], (s, (h + k) % hn))

    def lend_mate(c):
        q_swap(c).wait_recv()
        g_swap(c).wait_recv()
        q_lend(c, 1).start()
        g_lend(c, 1).start()

    def enter():
        loads = [
            pltpu.make_async_copy(src, dst, in_ls.at[k])
            for k, (src, dst) in enumerate(((lat_hbm, lat_ref), (qid_hbm, qid_ref)))
        ]
        for load in loads:
            load.start()
        barrier = pltpu.get_barrier_semaphore()

        def greet(to):
            pl.semaphore_signal(barrier, inc=1, device_id=to, device_id_type=MESH)

        greet((mate, h))
        for k in range(1, BACK + 1):
            @pl.when(z + k < line)
            def _():
                greet((s + 2 * k, h))
                greet((mate + 2 * k, h))

            @pl.when(z - k >= 0)
            def _():
                greet((s - 2 * k, h))
                greet((mate - 2 * k, h))
        for k in range(1, hn):
            greet((s, (h + k) % hn))
        for load in loads:
            load.wait()
        ids = jnp.transpose(jnp.broadcast_to(qid_ref[...].astype(F32), (tok, tok)))
        mine = jnp.transpose(lat_ref[...].astype(F32))
        packed = jnp.concatenate([mine, ids[:, :lat_all.shape[3] - width]], axis=1).astype(BF16)
        lat_all[2] = packed.reshape(lat_all.shape[1:])
        pl.semaphore_wait(barrier, 2 * (jnp.minimum(z, BACK) + jnp.minimum(line - 1 - z, BACK)) + hn)
        la_copy(0).start()
        for k in FAR:
            @pl.when(sends_to(k))
            def _():
                la_copy(k).start()

        def fetch(c):
            w_copy(c, 0).start()
            w_copy(c, 1).start()
            q_own(c).start()
            g_own(c).start()

        def swap(c):
            q_swap(c).start()
            g_swap(c).start()

        @pl.when(edge)
        def _():
            swap(0)
            for c in range(lent):
                q_lend(c, 0).start()
                g_lend(c, 0).start()
            for c in range(lent, chunks):
                fetch(c)

        @pl.when(inner)
        def _():
            for c in order:
                fetch(c)
            swap(order[0])

        lgacc[...] = jnp.zeros_like(lgacc)
        zero = jnp.zeros(part.shape[1:], BF16)

        def clear(i, c):
            part[i] = zero
            return c

        lax.fori_loop(0, chunks, clear, 0)
        for cond, buf, d, count in (
            (low, rzp, 0, chunks), (borrows_low, rzp, 1, lent),
            (high, rzm, line - 1, chunks), (borrows_high, rzm, line - 2, lent),
        ):
            @pl.when(cond)
            def _():
                for i in range(count):
                    buf[i, d] = jnp.zeros(buf.shape[2:], BF16)

        for k in FAR:
            @pl.when(gets_from(k))
            def _():
                la_copy(k).wait_recv()
                lb_copy(k).start()
                lc_copy(2 * (k + 1), core).start()

            @pl.when(jnp.logical_not(gets_from(k)))
            def _():
                for b in (2 * (k + 1), 2 * (k + 1) + 1):
                    lat_all[b] = jnp.zeros(lat_all.shape[1:], BF16)
        la_copy(0).wait_recv()
        lc_copy(3, core).start()
        for k in FAR:
            @pl.when(gets_from(k))
            def _():
                lb_copy(k).wait_recv()
                lc_copy(2 * (k + 1) + 1, core).start()

        @pl.when(edge)
        def _():
            for c in range(max(lent, plain)):
                if c < plain:
                    swap(lent + c)
                if c + 1 < lent:
                    swap(c + 1)
            lend_mate(0)

        @pl.when(inner)
        def _():
            for c in order[1:]:
                swap(c)

        lc_copy(3, 1 - core).wait_recv()
        for k in FAR:
            @pl.when(gets_from(k))
            def _():
                lc_copy(2 * (k + 1), 1 - core).wait_recv()
                lc_copy(2 * (k + 1) + 1, 1 - core).wait_recv()
        for b in range(SPAN):
            rows = lat_all[b].reshape(tok, lat_all.shape[3])
            lat_t[:, b * tok:(b + 1) * tok] = jnp.transpose(rows[:, :LATENT])

        def ids_of(b):
            tail = lat_all[b].reshape(tok, lat_all.shape[3])[:, LATENT:].astype(F32)
            return jnp.transpose(tail)[ROPE:ROPE + 1, :]

        row = lax.broadcasted_iota(jnp.int32, (tok, tok), 0)
        col = lax.broadcasted_iota(jnp.int32, (tok, tok), 1)

        def mask(which, window, query_at, shift):
            for k in range(2):
                query_id = ids_of(query_at + k)
                for b in range(BLOCKS):
                    back = window // 2 - 1 + b // 2
                    block = (s if b % 2 == 0 else mate) - 2 * back
                    rows = lat_all[window + b].reshape(tok, lat_all.shape[3])
                    key_id = rows[:, width:width + 1].astype(F32)
                    first = (s if k == 0 else mate) + shift - block
                    visible = (row <= col + first * tok) & (block >= 0) & (key_id == query_id)
                    bias[which, b * tok:(b + 1) * tok, k * tok:(k + 1) * tok] = jnp.where(visible, 0.0, -jnp.inf)

        mask(0, 2, 2, 0)

        @pl.when(borrows_low)
        def _():
            mask(1, 2, 4, -2)

        @pl.when(borrows_high)
        def _():
            mask(1, 0, 0, 2)

    def compute(c, is_lent):
        slot = jnp.where(is_lent, chunks + c, c)
        which = jnp.where(is_lent, 1, 0)
        window = jnp.where(is_lent & borrows_high, 0, 2)

        @pl.when(jnp.logical_not(is_lent))
        def _():
            w_copy(c, 0).wait()
            w_copy(c, 1).wait()
            q_own(c).wait()
            g_own(c).wait()
            q_swap(c).wait_recv()
            g_swap(c).wait_recv()

        @pl.when(is_lent)
        def _():
            for k in range(2):
                q_lend(c, k).wait_recv()
                g_lend(c, k).wait_recv()

        rows = lat_all[pl.ds(window, BLOCKS)].reshape(keys, lat_all.shape[3])
        lat = rows[:, :LATENT]
        rope = rows[:, LATENT:width]
        w = wb[c]
        q2 = qb[slot].reshape(queries, QW)
        g2 = gb[slot].reshape(queries, GW)
        kv = dot(lat, w, 1, 0).astype(BF16)
        dks, dvs, rope_sum = [], [], None
        for a in range(PAIR):
            q = q2[:, a * (NOPE + ROPE):(a + 1) * (NOPE + ROPE)]
            g = g2[:, a * VDIM:(a + 1) * VDIM]
            v = kv[:, PAIR * NOPE + a * VDIM:PAIR * NOPE + (a + 1) * VDIM]
            k = jnp.concatenate([kv[:, a * NOPE:(a + 1) * NOPE], rope], axis=1)
            sc = dot(k, q, 1, 1) * (scale * to_log2) + bias[which]
            e = jnp.exp2(sc - jnp.max(sc, axis=0, keepdims=True))
            p = e * (1.0 / jnp.sum(e, axis=0, keepdims=True))
            pb = p.astype(BF16)
            att = jnp.transpose(dot(v, pb, 0, 0)).astype(BF16)
            for k in range(2):
                atts[slot, k, :, a * VDIM:(a + 1) * VDIM] = att[k * tok:(k + 1) * tok]
            dp = dot(v, g, 1, 1)
            delta = jnp.sum(p * dp, axis=0, keepdims=True)
            ds = (p * (dp - delta) * scale).astype(BF16)
            dk = dot(ds, q, 1, 0)
            dvs.append(dot(pb, g, 1, 0).astype(BF16))
            dks.append(dk[:, :NOPE].astype(BF16))
            r = dk[:, NOPE:]
            rope_sum = r if rope_sum is None else rope_sum + r
        dd = jnp.concatenate(dks + dvs, axis=1)
        lat_cols = lat_t[:, pl.ds(pl.multiple_of(window * tok, 128), keys)]
        grad = dot(lat_cols, dd, 1, 0).reshape(part.shape[1:])
        part[c] = (part[c].astype(F32) + grad).astype(BF16)
        flat = (BLOCKS,) + lgacc.shape[1:4]
        at = pl.ds(window, BLOCKS)
        lgacc[at, :, :, :, :LATENT] += dot(dd, w, 1, 1).reshape(*flat, LATENT)
        lgacc[at, :, :, :, LATENT:] += rope_sum.reshape(*flat, ROPE)

        @pl.when(is_lent)
        def _():
            for k in range(2):
                a_lent(c, k).start()

        @pl.when(jnp.logical_not(is_lent))
        def _():
            a_swap(c, y).start()
            att_ref[:, cols(y, c, GW)] = atts[c, 0]

    def pass_on(i, r, up, first):
        d = line - 1 - r if up else r

        @pl.when(jnp.logical_not(first))
        def _():
            z_copy(i, d, up).wait_recv()
            buf = rzp if up else rzm
            part[i, d] = (part[i, d].astype(F32) + buf[i, d].astype(F32)).astype(BF16)

        z_copy(i, d, up).start()

    def pass_range(i, r0, r1, up, first):
        def one(r, c):
            pass_on(i, r, up, first)
            return c

        lax.fori_loop(r0, r1, one, 0)

    def pass_late(k0, k1, up):
        def one(k, c):
            pass_on(chunks - late + k % late, k // late, up, True)
            return c

        lax.fori_loop(k0, k1, one, 0)

    def relay(j, up):
        pos = z if up else line - 1 - z
        reach = line - 1 - pos
        t = j - 2 * (pos - 1)

        @pl.when(pos == 0)
        def _():
            @pl.when(j < plain - late)
            def _():
                pass_range(lent + j, 0, line - 1, up, True)

            @pl.when(j == plain - 1)
            def _():
                pass_late(0, late, up)

            @pl.when(j == plain + 1)
            def _():
                pass_late(late, late * (line - 1), up)

        @pl.when(pos > 0)
        def _():
            lead = jnp.int32(0)
            for c in range(lent):
                lead = jnp.where(t == ready[c], c + 1, lead)

            @pl.when(lead > 0)
            def _():
                pass_range(lead - 1, 0, reach, up, pos == 1)

            near, nearer = jnp.int32(0), jnp.int32(0)
            for c in range(lent, chunks - late):
                near = jnp.where(t == ready[c], c + 1, near)
                nearer = jnp.where(t == ready[c] + 1, c + 1, nearer)

            @pl.when((near > 0) & (reach > 0))
            def _():
                pass_on(near - 1, 0, up, False)

            @pl.when(nearer > 0)
            def _():
                pass_range(nearer - 1, 1, reach, up, False)

            k = t - (work - 1)

            @pl.when((k >= 0) & (k < late * reach))
            def _():
                pass_on(chunks - late + k % late, k // late, up, False)

    def finish(i):
        @pl.when(jnp.logical_not(low) & jnp.logical_not(borrows_low & (i < lent)))
        def _():
            z_copy(i, z, True).wait_recv()

        @pl.when(jnp.logical_not(high) & jnp.logical_not(borrows_high & (i < lent)))
        def _():
            z_copy(i, z, False).wait_recv()

        def total(yy):
            return part[i, z, yy].astype(F32) + rzp[i, z, yy].astype(F32) + rzm[i, z, yy].astype(F32)

        part[i, z, other] = total(other).astype(BF16)
        y_copy(i).start()
        put(i, y, total(y))

    def put(i, half, rows):
        kwg_ref[:, cols(half, i, PAIR * NOPE)] = rows[:, :PAIR * NOPE]
        vwg_ref[:, cols(half, i, GW)] = rows[:, PAIR * NOPE:]

    def close(i, carry):
        y_copy(i).wait_recv()
        put(i, other, yr[i].astype(F32))
        return carry

    def latent_twin():
        l1s[...] = lgacc[:, :, 1 - core].astype(BF16)
        l1_copy().start()

    def latent_send():
        l1_copy().wait_recv()
        twos[...] = lgacc[:, :, core] + l1r[...].astype(F32)
        for k in range(1, chips):
            xs[k - 1] = twos[:, (chip + k) % chips].astype(BF16)
        for p in PAIRS:
            @pl.when(gets_from(p - 1))
            def _():
                for k in range(1, chips):
                    x_copy(k, p).start()

    def latent_pass():
        for p in PAIRS:
            @pl.when(gets_from(p - 1))
            def _():
                for k in range(1, chips):
                    x_copy(k, p).wait_recv()
                for b in (2 * p, 2 * p + 1):
                    tot = twos[b, chip]
                    for k in range(1, chips):
                        tot = tot + xr[k - 1, b].astype(F32)
                    if b == 2:
                        lgown[...] = tot
                    else:
                        l2s[b] = tot.astype(BF16)
                        l2_copy(b).start()

    def latent_gather():
        for b in range(SPAN):
            if b != 2:
                @pl.when(sends_to(b // 2 - 1))
                def _():
                    l2_copy(b).wait_recv()
                    lgown[...] += l2r[b].astype(F32)
        hb[h] = lgown[...].astype(BF16)
        for k in range(1, hn):
            h_copy(k, h).start()

    def latent_out():
        for k in range(1, hn):
            h_copy(k, (h + k) % hn).wait_recv()
        lg_ref[...] = jnp.transpose(hb[...].astype(F32).reshape(tok, width))

    enter()
    last = max(done.values()) + 1

    def turn(j, carry):
        c = jnp.where(edge, lent + j, pick([c for c, _ in turns], j))
        is_lent = inner & (pick([f for _, f in turns], j) > 0)
        active = (j < jnp.where(edge, plain, work)) & (borrows | jnp.logical_not(is_lent))

        @pl.when(active)
        def _():
            compute(c, is_lent)

        @pl.when(edge & (j < lent - 1))
        def _():
            lend_mate(j + 1)

        spent = jnp.where(edge, plain - 1, work - 1)

        @pl.when(j == spent)
        def _():
            latent_twin()

        @pl.when(j == spent + 1)
        def _():
            latent_send()

        @pl.when((j == spent + 2) & edge)
        def _():
            latent_pass()

        for up in (True, False):
            relay(j, up)

        @pl.when((j == spent + late * (line - 2) - 1) & inner)
        def _():
            latent_pass()

        fin = jnp.int32(0)
        for i in range(chunks):
            fin = jnp.where(j == done[i], i + 1, fin)

        @pl.when(fin > 0)
        def _():
            finish(fin - 1)

        @pl.when(edge & (fin > 0) & (fin <= lent))
        def _():
            for k in range(2):
                a_lent(fin - 1, k).wait_recv()
            a_swap(fin - 1, y).start()
            att_ref[:, cols(y, fin - 1, GW)] = atts[fin - 1, 0]

        @pl.when(j == last - late - 1)
        def _():
            lax.fori_loop(0, chunks - late, close, 0)

        return carry

    lax.fori_loop(0, last, turn, 0)
    latent_gather()
    lax.fori_loop(chunks - late, chunks, close, 0)
    latent_out()

    for k in range(1, hn):
        h_copy(k, h).wait_send()
    l1_copy().wait_send()
    for k in range(1, chips):
        for p in PAIRS:
            @pl.when(gets_from(p - 1))
            def _():
                x_copy(k, p).wait_send()
    for b in range(SPAN):
        if b != 2:
            @pl.when(gets_from(b // 2 - 1))
            def _():
                l2_copy(b).wait_send()

    def drain(j, carry):
        y_copy(j).wait_send()
        a_swap(j, other).wait_recv()
        a_swap(j, y).wait_send()
        q_swap(j).wait_send()
        g_swap(j).wait_send()
        for d in range(line):
            @pl.when((d > z) & jnp.logical_not(low & (j < lent)))
            def _():
                z_copy(j, d, True).wait_send()

            @pl.when((d < z) & jnp.logical_not(high & (j < lent)))
            def _():
                z_copy(j, d, False).wait_send()
        return carry

    lax.fori_loop(0, chunks, drain, 0)
    for c in range(lent):
        for k in range(2):
            @pl.when(edge)
            def _():
                q_lend(c, k).wait_send()
                g_lend(c, k).wait_send()

            @pl.when(borrows)
            def _():
                a_lent(c, k).wait_send()
    la_copy(0).wait_send()
    lc_copy(3, core).wait_send()
    for k in FAR:
        @pl.when(sends_to(k))
        def _():
            la_copy(k).wait_send()

        @pl.when(gets_from(k))
        def _():
            lb_copy(k).wait_send()
            lc_copy(2 * (k + 1), core).wait_send()
            lc_copy(2 * (k + 1) + 1, core).wait_send()


def flush(*refs):
    sems = refs[-1]
    copies = [pltpu.make_async_copy(refs[k], refs[4 + k], sems.at[k]) for k in range(4)]
    for copy in copies:
        copy.start()
    for copy in copies:
        copy.wait()


def per_device(n, hn, queries, latents, doc_ids, key_weight, value_weight, out_grad):
    tok = latents.shape[0]
    heads = key_weight.shape[1] // NOPE
    chunks = heads // 2 // PAIR
    line = n // 2
    rows = LATENT // n
    lent = plan(chunks, line)[0]
    slots = chunks + lent
    keys = BLOCKS * tok
    width = LATENT + ROPE
    wide = width + 64
    share = tok // hn
    chips = hn // 2
    ids = doc_ids.reshape(1, tok)
    whole = pl.BlockSpec(memory_space=pltpu.VMEM)
    far = pl.BlockSpec(memory_space=pltpu.HBM)
    dma = pltpu.SemaphoreType.DMA
    ring = max(chips - 1, 1)
    att, lg, kwg, vwg = pl.pallas_call(
        functools.partial(kernel, n, hn, chunks),
        out_shape=(
            pltpu.VMEM((tok, heads * VDIM), BF16),
            pltpu.VMEM((width, tok), F32),
            pltpu.VMEM((rows, heads * NOPE), F32),
            pltpu.VMEM((rows, heads * VDIM), F32),
        ),
        in_specs=[far] * 6,
        out_specs=(whole, whole, whole, whole),
        scratch_shapes=[
            pltpu.VMEM((width, tok), BF16),
            pltpu.VMEM((1, tok), jnp.int32),
            pltpu.VMEM((SPAN, 2, tok // 2, wide), BF16),
            pltpu.VMEM((LATENT, SPAN * tok), BF16),
            pltpu.VMEM((2, keys, 2 * tok), F32),
            pltpu.VMEM((SPAN, chips, 2, share, width), F32),
            pltpu.VMEM((chunks, LATENT, WW), BF16),
            pltpu.VMEM((slots, 2, tok, QW), BF16),
            pltpu.VMEM((slots, 2, tok, GW), BF16),
            pltpu.VMEM((slots, 2, tok, GW), BF16),
            pltpu.VMEM((chunks, line, 2, rows, WW), BF16),
            pltpu.VMEM((chunks, line, 2, rows, WW), BF16),
            pltpu.VMEM((chunks, line, 2, rows, WW), BF16),
            pltpu.VMEM((chunks, rows, WW), BF16),
            pltpu.VMEM((SPAN, chips, share, width), BF16),
            pltpu.VMEM((SPAN, chips, share, width), BF16),
            pltpu.VMEM((SPAN, chips, share, width), F32),
            pltpu.VMEM((ring, SPAN, share, width), BF16),
            pltpu.VMEM((ring, SPAN, share, width), BF16),
            pltpu.VMEM((SPAN, share, width), BF16),
            pltpu.VMEM((SPAN, share, width), BF16),
            pltpu.VMEM((share, width), F32),
            pltpu.VMEM((hn, share, width), BF16),
            dma((2,)), dma((chunks, 2)), dma((chunks,)), dma((chunks,)),
            dma((chunks,)), dma((chunks,)), dma((chunks,)), dma((chunks,)),
            dma((lent, 2)), dma((lent, 2)), dma((lent, 2)), dma((lent, 2)),
            dma((slots, 2)), dma((chunks,)), dma((lent, 2)),
            dma((BACK + 2,)), dma((BACK + 2,)), dma((BACK + 2,)), dma((BACK + 2,)), dma((SPAN,)), dma((SPAN,)),
            dma((chunks, line)), dma((chunks, line)), dma((chunks, line)), dma((chunks, line)),
            dma((chunks,)), dma((chunks,)),
            dma((1,)), dma((1,)), dma((ring, SPAN // 2)), dma((ring, SPAN // 2)), dma((SPAN,)), dma((SPAN,)),
            dma((max(hn - 1, 1),)), dma((hn,)),
        ],
        compiler_params=pltpu.CompilerParams(
            collective_id=0,
            has_side_effects=True,
            vmem_limit_bytes=VMEM_LIMIT,
        ),
    )(latents.T, ids, queries, out_grad, key_weight, value_weight)
    out = (att, lg, kwg, vwg)
    att, lg, kwg, vwg = pl.pallas_call(
        flush,
        out_shape=tuple(pltpu.HBM(o.shape, o.dtype) for o in out),
        in_specs=[whole] * 4,
        out_specs=(far,) * 4,
        scratch_shapes=[dma((4,))],
        compiler_params=pltpu.CompilerParams(vmem_limit_bytes=1024 * 1024),
    )(*out)
    return att, lg.T, kwg, vwg


def solution(mesh):
    in_specs = (
        P("seq", "head"),
        P("seq", None),
        P("seq"),
        P(None, "head"),
        P(None, "head"),
        P("seq", "head"),
    )
    out_specs = (P("seq", "head"), P("seq", None), P("seq", "head"), P("seq", "head"))
    body = functools.partial(per_device, mesh.shape["seq"], mesh.shape["head"])
    return jax.shard_map(
        body, mesh=mesh, in_specs=in_specs, out_specs=out_specs, check_vma=False
    )
```

time: 108 us -> 90.3 us (0.84)
  Pallas kernels: 107 us -> 89.5 us
    pallas_call x1, Pallas kernels: 105 us -> 87.7 us  [per_device(): pl.pallas_call(functools.partial(kernel, n, hn, chunks), out_shape=(pltpu...]
where the time goes in v3:
time: 90.3 us; the launch traced here: 90.2 us
  Pallas kernels  89.5 us (99%)
    pallas_call x1, Pallas kernels, per_device(): pl.pallas_call(functools.partial(kernel, n, hn, chunks), out_shape=(pltpu...  87.7 us

profile of v3, /device:TPU:0, one launch (start us, length us, event | category | flops | bytes accessed | tf_op | source)
XLA Modules:
  0.0 90.2 jit_solution(9016121327430390843)
XLA Ops:
  0.6 87.7 %shard_map.93 = (bf16[128,4096]{1,0:T(8,128)(2,1)S(1)}, f32[576,128]{1,0:T(8,128)S(1)}, f32[64,4096]{1,0:T(8,128)S(1)}, f32[64,4096]{1,0:T(8,128)S(1)}) custom-call(bf16[576,128]{1,0:T(8,128)(2,1)} %bitcast.3, s32[1,128]{1,0:T(1,128)} %bitcast.4, bf16[128,6144]{1,0:T(8,128)(2,1)} %q_ref.1, bf16[128,4096]{1,0:T(8,128)(2,1)} %g_ref.1, ...), custom_call_target="tpu_custom_call" | custom-call | tf_op jit(solution)/shard_map/pallas_call | solution.py:698
  88.4 1.8 %shard_map.94 = (bf16[128,4096]{1,0:T(8,128)(2,1)}, f32[576,128]{1,0:T(8,128)}, f32[64,4096]{1,0:T(8,128)}, f32[64,4096]{1,0:T(8,128)}) custom-call(bf16[128,4096]{1,0:T(8,128)(2,1)S(1)} %get-tuple-element.12.refs_0_, f32[576,128]{1,0:T(8,128)S(1)} %get-tuple-element.13.refs_1_, f32[64,4096]{1,0:T(8,128)S(1)} %get-tuple-element.14.refs_2_, ...), custom_call_target="tpu_custom_call" | custom-call | tf_op jit(solution)/shard_map/pallas_call | solution.py:749

commit v4 on v3

--- a/solution.py
+++ b/solution.py
@@ -59,6 +59,7 @@
     for c in range(chunks):
         late_rank = c - (chunks - late)
         done[c] = ready[c] + 2 * (line - 2) if late_rank < 0 else tail + late_rank
+    assert len(set(done.values())) == chunks
     return lent, plain, late, turns, ready, [c for _, c in order], done
 
 
@@ -175,7 +176,10 @@
 
     def l2_copy(b):
         base = s if b % 2 == 0 else mate
-        return remote(l2s.at[b], l2r.at[b], l2_ss.at[b], l2_rs.at[b], (base - 2 * (b // 2 - 1), h))
+        hops = b // 2 - 1
+        if b >= SPAN - 2:
+            base, hops = jnp.where(high, s, base), jnp.where(high, 1, hops)
+        return remote(l2s.at[b], l2r.at[b], l2_ss.at[b], l2_rs.at[b], (base - 2 * hops, h))
 
     def h_copy(k, slot):
         return remote(hb.at[slot], hb.at[slot], h_ss.at[k - 1], h_rs.at[slot], (s, (h + k) % hn))
@@ -236,8 +240,8 @@
 
         @pl.when(edge)
         def _():
-            swap(0)
-            for c in range(lent):
+            q_swap(0).start()
+            for c in range(min(2, lent)):
                 q_lend(c, 0).start()
                 g_lend(c, 0).start()
             for c in range(lent, chunks):
@@ -247,7 +251,7 @@
         def _():
             for c in order:
                 fetch(c)
-            swap(order[0])
+            q_swap(order[0]).start()
 
         lgacc[...] = jnp.zeros_like(lgacc)
         zero = jnp.zeros(part.shape[1:], BF16)
@@ -277,6 +281,7 @@
             def _():
                 for b in (2 * (k + 1), 2 * (k + 1) + 1):
                     lat_all[b] = jnp.zeros(lat_all.shape[1:], BF16)
+        g_swap(0).start()
         la_copy(0).wait_recv()
         lc_copy(3, core).start()
         for k in FAR:
@@ -293,6 +298,9 @@
                 if c + 1 < lent:
                     swap(c + 1)
             lend_mate(0)
+            for c in range(2, lent):
+                q_lend(c, 0).start()
+                g_lend(c, 0).start()
 
         @pl.when(inner)
         def _():
@@ -443,11 +451,7 @@
 
             @pl.when(j == plain - 1)
             def _():
-                pass_late(0, late, up)
-
-            @pl.when(j == plain + 1)
-            def _():
-                pass_late(late, late * (line - 1), up)
+                pass_late(0, late * (line - 1), up)
 
         @pl.when(pos > 0)
         def _():
@@ -530,6 +534,16 @@
                         tot = tot + xr[k - 1, b].astype(F32)
                     if b == 2:
                         lgown[...] = tot
+                    elif 2 * p == SPAN - 4:
+                        @pl.when(borrows_high)
+                        def _():
+                            l2_copy(b + 2).wait_recv()
+                            l2s[b] = (tot + l2r[b + 2].astype(F32)).astype(BF16)
+
+                        @pl.when(jnp.logical_not(borrows_high))
+                        def _():
+                            l2s[b] = tot.astype(BF16)
+                        l2_copy(b).start()
                     else:
                         l2s[b] = tot.astype(BF16)
                         l2_copy(b).start()
@@ -537,7 +551,9 @@
     def latent_gather():
         for b in range(SPAN):
             if b != 2:
-                @pl.when(sends_to(b // 2 - 1))
+                last_hop = z != line - 3 if b >= SPAN - 2 else z >= 0
+
+                @pl.when(sends_to(b // 2 - 1) & last_hop)
                 def _():
                     l2_copy(b).wait_recv()
                     lgown[...] += l2r[b].astype(F32)
@@ -572,7 +588,7 @@
         def _():
             latent_twin()
 
-        @pl.when(j == spent + 1)
+        @pl.when((j == spent + 1) & edge)
         def _():
             latent_send()
 
@@ -583,7 +599,11 @@
         for up in (True, False):
             relay(j, up)
 
-        @pl.when((j == spent + late * (line - 2) - 1) & inner)
+        @pl.when((j == spent + 1) & inner)
+        def _():
+            latent_send()
+
+        @pl.when((j == spent + late * (line - 2)) & inner)
         def _():
             latent_pass()
 

time: 90.3 us -> 88.5 us (0.980)
  Pallas kernels: 89.5 us -> 87.7 us
    pallas_call x1, Pallas kernels: 87.7 us -> 85.9 us  [per_device(): pl.pallas_call(functools.partial(kernel, n, hn, chunks), out_shape=(pltpu...]
where the time goes in v4:
time: 88.5 us; the launch traced here: 88.3 us
  Pallas kernels  87.7 us (99%)
    pallas_call x1, Pallas kernels, per_device(): pl.pallas_call(functools.partial(kernel, n, hn, chunks), out_shape=(pltpu...  85.9 us
    pallas_call x1, Pallas kernels, per_device(): pl.pallas_call(flush, out_shape=tuple((pltpu.HBM(o.shape, o.dtype) for o...  1.8 us

profile of v4, /device:TPU:0, one launch (start us, length us, event | category | flops | bytes accessed | tf_op | source)
XLA Modules:
  0.0 88.3 jit_solution(1395585526112200385)
XLA Ops:
  0.6 85.9 %shard_map.93 = (bf16[128,4096]{1,0:T(8,128)(2,1)S(1)}, f32[576,128]{1,0:T(8,128)S(1)}, f32[64,4096]{1,0:T(8,128)S(1)}, f32[64,4096]{1,0:T(8,128)S(1)}) custom-call(bf16[576,128]{1,0:T(8,128)(2,1)} %bitcast.3, s32[1,128]{1,0:T(1,128)} %bitcast.4, bf16[128,6144]{1,0:T(8,128)(2,1)} %q_ref.1, bf16[128,4096]{1,0:T(8,128)(2,1)} %g_ref.1, ...), custom_call_target="tpu_custom_call" | custom-call | tf_op jit(solution)/shard_map/pallas_call | solution.py:718
  86.5 1.8 %shard_map.94 = (bf16[128,4096]{1,0:T(8,128)(2,1)}, f32[576,128]{1,0:T(8,128)}, f32[64,4096]{1,0:T(8,128)}, f32[64,4096]{1,0:T(8,128)}) custom-call(bf16[128,4096]{1,0:T(8,128)(2,1)S(1)} %get-tuple-element.12.refs_0_, f32[576,128]{1,0:T(8,128)S(1)} %get-tuple-element.13.refs_1_, f32[64,4096]{1,0:T(8,128)S(1)} %get-tuple-element.14.refs_2_, ...), custom_call_target="tpu_custom_call" | custom-call | tf_op jit(solution)/shard_map/pallas_call | solution.py:769

commit v5 on v4

--- a/solution.py
+++ b/solution.py
@@ -58,7 +58,7 @@
     done = {}
     for c in range(chunks):
         late_rank = c - (chunks - late)
-        done[c] = ready[c] + 2 * (line - 2) if late_rank < 0 else tail + late_rank
+        done[c] = ready[c] + 2 * (line - 2) + 1 if late_rank < 0 else tail + late_rank
     assert len(set(done.values())) == chunks
     return lent, plain, late, turns, ready, [c for _, c in order], done
 
@@ -603,7 +603,7 @@
         def _():
             latent_send()
 
-        @pl.when((j == spent + late * (line - 2)) & inner)
+        @pl.when((j == spent + late * (line - 2) - 2) & inner)
         def _():
             latent_pass()
 

time: 88.5 us -> 89.1 us (level)
  the two profiles are of different devices: /device:TPU:0 before, /device:TPU:17 now
where the time goes in v5:
time: 89.1 us; the launch traced here: 89 us
  Pallas kernels  88.3 us (99%)
    pallas_call x1, Pallas kernels, per_device(): pl.pallas_call(functools.partial(kernel, n, hn, chunks), out_shape=(pltpu...  86.5 us
    pallas_call x1, Pallas kernels, per_device(): pl.pallas_call(flush, out_shape=tuple((pltpu.HBM(o.shape, o.dtype) for o...  1.8 us

profile of v5, /device:TPU:17, one launch (start us, length us, event | category | flops | bytes accessed | tf_op | source)
XLA Modules:
  0.0 89.0 jit_solution(8577139798891448825)
XLA Ops:
  0.6 86.5 %shard_map.93 = (bf16[128,4096]{1,0:T(8,128)(2,1)S(1)}, f32[576,128]{1,0:T(8,128)S(1)}, f32[64,4096]{1,0:T(8,128)S(1)}, f32[64,4096]{1,0:T(8,128)S(1)}) custom-call(bf16[576,128]{1,0:T(8,128)(2,1)} %bitcast.3, s32[1,128]{1,0:T(1,128)} %bitcast.4, bf16[128,6144]{1,0:T(8,128)(2,1)} %q_ref.1, bf16[128,4096]{1,0:T(8,128)(2,1)} %g_ref.1, ...), custom_call_target="tpu_custom_call" | custom-call | tf_op jit(solution)/shard_map/pallas_call | solution.py:718
  87.2 1.8 %shard_map.94 = (bf16[128,4096]{1,0:T(8,128)(2,1)}, f32[576,128]{1,0:T(8,128)}, f32[64,4096]{1,0:T(8,128)}, f32[64,4096]{1,0:T(8,128)}) custom-call(bf16[128,4096]{1,0:T(8,128)(2,1)S(1)} %get-tuple-element.12.refs_0_, f32[576,128]{1,0:T(8,128)S(1)} %get-tuple-element.13.refs_1_, f32[64,4096]{1,0:T(8,128)S(1)} %get-tuple-element.14.refs_2_, ...), custom_call_target="tpu_custom_call" | custom-call | tf_op jit(solution)/shard_map/pallas_call | solution.py:769
